TPU v7x, 32 devices: a whole 2x2x4 slice. The times are simulated.
32 devices in a mesh: groups: 2 (over x), hid: 16 (over z, y, core).
Axes of the slice: x: 2, y: 2, z: 4, core: 2. Of those that a mesh axis runs over, the one named last changes fastest.
Arguments:
- queries: bfloat16 [128, 64, 128], P(('groups', 'hid')), parts along dimension 0, may hold values from -12 to 12
- k_cache: bfloat16 [128, 192, 1024], P(('groups', 'hid')), parts along dimension 0, may hold values from -450 to 450
- v_cache: bfloat16 [128, 192, 1024], P(('groups', 'hid')), parts along dimension 0, may hold values from -6 to 6
- lengths: int32 [128], P(('groups', 'hid')), parts along dimension 0, may hold values from 24 to 192, as said below
- residual_in: bfloat16 [128, 8192], P(('groups', 'hid')), parts along dimension 0, may hold values from -6 to 6
- norm_gain: float32 [8192], replicated, may hold values from 0.25 to 1.75
- gate_w: bfloat16 [16, 56, 1024, 128], P('hid'), may hold values from -0.0625 to 0.0625
- up_w: bfloat16 [16, 56, 1024, 128], P('hid'), may hold values from -0.0625 to 0.0625
- down_w: bfloat16 [16, 56, 128, 1024], P('hid'), may hold values from -0.09375 to 0.09375
- block_list: int32 [4, 28], P('groups'), parts along dimension 0, may hold values from 0 to 55, as said below
- block_count: int32 [4], P('groups'), parts along dimension 0, may hold values from 1 to 28, as said below
Outputs:
- layer_out: bfloat16 [128, 8192], P(('groups', 'hid')), parts along dimension 0
There are 2 independent parts, one for each index of `groups`. A program takes and returns all parts, laid end to end along the dimension named above; an argument that names none is the same for every part. Nothing has to cross between parts.
Inputs may be any that keep to these rules, and one draw needn't show every extreme that they name: `lengths`: some request's length is 192. `block_list`: each row holds 28 distinct block indices of its group. `block_count`: exactly one group has all 28 listed blocks active.
All inputs are finite; a program needn't handle non-finite values.
Results may differ from a plain program's by a relative error of at most 0.006.
Values may be sent and summed in bfloat16 or wider, within the bound.
A program may use at most 128 MiB of HBM per device.

v0:
```python
import functools
import math

import jax
import jax.numpy as jnp
from jax import lax
from jax.experimental import pallas as pl
from jax.experimental.pallas import tpu as pltpu
from jax.sharding import PartitionSpec as P

MESH = pl.DeviceIdType.MESH
F32 = jnp.float32
BF16 = jnp.bfloat16
LAG_ADD, LAG_HID, LAG_FWD, LAG_DOWN = 1, 5, 9, 11


def layer_kernel(
    dims,
    lengths_ref,
    list_ref,
    count_ref,
    q_hbm,
    res_hbm,
    gain_hbm,
    k_hbm,
    v_hbm,
    gate_hbm,
    up_hbm,
    down_hbm,
    out_ref,
    q_ref,
    res_ref,
    gain_ref,
    k_vm,
    v_vm,
    gate_vm,
    up_vm,
    down_vm,
    mixed,
    send_x,
    arrived,
    wide,
    x_vm,
    pair_out,
    pair_in,
    chip_out,
    chip_in,
    hid_all,
    acc,
    ret_out,
    ret_in,
    small_sem,
    kv_sem,
    w_sem,
    a2a_s,
    a2a_r,
    pair_s,
    pair_r,
    chip_s,
    chip_r,
    hid_s,
    hid_r,
    fwd_s,
    fwd_r,
    ret_s,
    ret_r,
):
    n, mdl, rows, heads, hd, kv, cache, width, bw, cap, cb, pieces = dims
    me = lax.axis_index("hid")
    group = me // mdl
    member = me % mdl
    base = group * mdl
    core = member % 2
    chip = member // 2
    chips = mdl // 2
    partner = base + chip * 2 + (1 - core)
    ds = width // mdl
    sub = ds // hd
    lanes = width // hd
    tile = rows * sub
    batch = rows * n
    rm = batch // mdl
    nch = cap // cb
    hpk = heads // kv
    blk_piece = gate_vm.shape[0] // pieces

    small = [
        pltpu.make_async_copy(src, dst, small_sem.at[i])
        for i, (src, dst) in enumerate(
            ((res_hbm, res_ref), (q_hbm, q_ref), (gain_hbm, gain_ref))
        )
    ]
    for copy in small:
        copy.start()
    kv_copies = []
    for r in range(rows):
        ck = pltpu.make_async_copy(k_hbm.at[r], k_vm.at[r], kv_sem.at[0, r])
        cv = pltpu.make_async_copy(v_hbm.at[r], v_vm.at[r], kv_sem.at[1, r])
        ck.start()
        cv.start()
        kv_copies.append((ck, cv))

    def weight_copy(which, hbm, vm, p):
        span = pl.ds(p * blk_piece, blk_piece)
        return pltpu.make_async_copy(hbm.at[0, span], vm.at[span], w_sem.at[which, p])

    barrier = pltpu.get_barrier_semaphore()

    def greet(d, carry):
        pl.semaphore_signal(
            barrier, inc=1, device_id={"hid": (me + d) % n}, device_id_type=MESH
        )
        return carry

    lax.fori_loop(1, n, greet, 0)

    for copy in small:
        copy.wait()
    for h in range(lanes):
        mixed[pl.ds(h, rows, stride=lanes), :] = res_ref[:, h * hd : (h + 1) * hd].astype(F32)

    slot = lax.broadcasted_iota(jnp.int32, (heads, cache), 1)
    q_rows = []
    for r in range(rows):
        q = q_ref[r].astype(F32)
        cols = []
        for k in range(kv):
            parts = []
            if k > 0:
                parts.append(jnp.zeros((k * hpk, hd), F32))
            parts.append(q[k * hpk : (k + 1) * hpk])
            if k < kv - 1:
                parts.append(jnp.zeros(((kv - 1 - k) * hpk, hd), F32))
            cols.append(jnp.concatenate(parts, axis=0).astype(BF16))
        q_rows.append(jnp.concatenate(cols, axis=1))
    for ck, cv in kv_copies:
        ck.wait()
        cv.wait()
    for p in range(pieces):
        weight_copy(0, gate_hbm, gate_vm, p).start()
        weight_copy(1, up_hbm, up_vm, p).start()
    scores = [
        lax.dot_general(
            q_rows[r], k_vm[r], (((1,), (1,)), ((), ())), preferred_element_type=F32
        ) * (1.0 / math.sqrt(hd))
        for r in range(rows)
    ]
    valid = [slot < lengths_ref[r] for r in range(rows)]
    scores = [jnp.where(valid[r], scores[r], -1e30) for r in range(rows)]
    tops = [jnp.max(v, axis=1, keepdims=True) for v in scores]
    terms = [jnp.where(valid[r], jnp.exp(scores[r] - tops[r]), 0.0) for r in range(rows)]
    sums = [jnp.sum(v, axis=1, keepdims=True) for v in terms]
    probs = [(terms[r] / sums[r]).astype(BF16) for r in range(rows)]
    mixed_rows = []
    for r in range(rows):
        wide_att = jnp.dot(probs[r], v_vm[r], preferred_element_type=F32)
        att = jnp.concatenate(
            [wide_att[k * hpk : (k + 1) * hpk, k * hd : (k + 1) * hd] for k in range(kv)], axis=0
        )
        mixed_rows.append(mixed[r * lanes : (r + 1) * lanes, :] + att)
    normed = []
    for r in range(rows):
        row = mixed_rows[r]
        mixed[r * lanes : (r + 1) * lanes, :] = row
        mean_sq = jnp.sum(jnp.sum(row * row, axis=1, keepdims=True), axis=0, keepdims=True) / width
        normed.append(row * lax.rsqrt(mean_sq + 1e-05) * gain_ref[...])
    for m in range(mdl):
        piece = jnp.concatenate([v[m * sub : (m + 1) * sub] for v in normed], axis=0)
        send_x[m] = piece.astype(BF16)

    pl.semaphore_wait(barrier, n - 1)

    def x_copy(d):
        to = (me + d) % n
        return pltpu.make_async_remote_copy(
            src_ref=send_x.at[to % mdl],
            dst_ref=arrived.at[me],
            send_sem=a2a_s.at[d],
            recv_sem=a2a_r.at[d],
            device_id={"hid": to},
            device_id_type=MESH,
        )

    def x_landed(d):
        return pltpu.make_async_remote_copy(
            src_ref=send_x.at[0],
            dst_ref=arrived.at[(me - d + n) % n],
            send_sem=a2a_s.at[d],
            recv_sem=a2a_r.at[d],
            device_id={"hid": (me - d + n) % n},
            device_id_type=MESH,
        )

    def loop(lo, hi, f):
        def body(i, carry):
            f(i)
            return carry

        lax.fori_loop(lo, hi, body, 0)

    loop(n // 2, n, lambda d: x_copy(d).start())
    loop(1, n // 2, lambda d: x_copy(d).start())
    arrived[me] = send_x[member]
    acc[...] = jnp.zeros_like(acc)
    loop(1, n, lambda d: x_landed(d).wait_recv())

    def widen(i):
        wide[pl.ds(pl.multiple_of(i * tile, tile), tile), :] = arrived[i].astype(F32)

    loop(0, n, widen)
    for j in range(sub):
        x_vm[:, j * hd : (j + 1) * hd] = wide[pl.ds(j, batch, stride=sub), :].astype(BF16)

    for p in range(pieces):
        weight_copy(0, gate_hbm, gate_vm, p).wait()
        weight_copy(1, up_hbm, up_vm, p).wait()
    for p in range(pieces):
        weight_copy(2, down_hbm, down_vm, p).start()

    def remote(src, dst, ss, rs, to):
        return pltpu.make_async_remote_copy(
            src_ref=src, dst_ref=dst, send_sem=ss, recv_sem=rs,
            device_id={"hid": to}, device_id_type=MESH,
        )

    def pair_copy(i):
        return remote(
            pair_out.at[i, 1 - core], pair_in.at[i], pair_s.at[i], pair_r.at[i], partner
        )

    def chip_copy(i, k):
        to = (chip + k) % chips
        return remote(
            chip_out.at[i, to], chip_in.at[i, k - 1], chip_s.at[i, k - 1], chip_r.at[i, k - 1],
            base + to * 2 + core,
        )

    def hid_copy(i, k):
        to = partner if k == 0 else base + ((chip + k) % chips) * 2 + core
        return remote(
            hid_all.at[member, i], hid_all.at[member, i], hid_s.at[i, k], hid_r.at[i, k], to
        )

    def hid_landed(i, k):
        whose = chip * 2 + 1 - core if k == 0 else ((chip - k + chips) % chips) * 2 + core
        return remote(
            hid_all.at[whose, i], hid_all.at[whose, i], hid_s.at[i, k], hid_r.at[i, k], partner
        )

    def fwd_copy(i, k):
        whose = ((chip - k + chips) % chips) * 2 + core
        return remote(
            hid_all.at[whose, i], hid_all.at[whose, i], fwd_s.at[i, k - 1], fwd_r.at[i, k - 1],
            partner,
        )

    def fwd_landed(i, k):
        whose = ((chip - k + chips) % chips) * 2 + 1 - core
        return remote(
            hid_all.at[whose, i], hid_all.at[whose, i], fwd_s.at[i, k - 1], fwd_r.at[i, k - 1],
            partner,
        )

    def project(i):
        x = x_vm[...]
        for pair in range(cb // 2):
            got = []
            for b in range(2):
                which = list_ref[group, i * cb + pair * 2 + b]
                w = jnp.concatenate([gate_vm[which], up_vm[which]], axis=1)
                got.append(jnp.dot(x, w, preferred_element_type=F32))
            for m in range(mdl):
                both = jnp.concatenate([y[m * rm : (m + 1) * rm] for y in got], axis=0)
                pair_out[i, m % 2, m // 2, pair * 2 * rm : (pair + 1) * 2 * rm, :] = both.astype(
                    BF16
                )
        pair_copy(i).start()

    def add_pair(i):
        pair_copy(i).wait_recv()
        for q in range(chips):
            total = pair_out[i, core, q].astype(F32) + pair_in[i, q].astype(F32)
            chip_out[i, q] = total.astype(BF16)
        for k in range(1, chips):
            chip_copy(i, k).start()

    def make_hidden(i):
        for k in range(1, chips):
            chip_copy(i, k).wait_recv()
        total = chip_out[i, chip].astype(F32)
        for k in range(1, chips):
            total = total + chip_in[i, k - 1].astype(F32)
        gate, up = total[:, :bw], total[:, bw:]
        row = lax.broadcasted_iota(jnp.int32, gate.shape, 0)
        active = row < (count_ref[group] - i * cb) * rm
        hid_all[member, i] = jnp.where(active, jnp.maximum(gate, 0.0) * up, 0.0).astype(BF16)
        for k in range(1, chips):
            hid_copy(i, k).start()
        hid_copy(i, 0).start()

    def forward(i):
        for k in range(1, chips):
            hid_landed(i, k).wait_recv()
            fwd_copy(i, k).start()

    def down(i):
        hid_landed(i, 0).wait_recv()
        for k in range(1, chips):
            fwd_landed(i, k).wait_recv()
        total = acc[...]
        for pair in range(cb // 2):
            parts = []
            for m in range(mdl):
                two = hid_all[m, i, pair * 2 * rm : (pair + 1) * 2 * rm, :].astype(F32)
                parts.append(jnp.concatenate([two[:rm], two[rm:]], axis=1))
            lhs = jnp.concatenate(parts, axis=0).astype(BF16)
            w = jnp.concatenate(
                [down_vm[list_ref[group, i * cb + pair * 2 + b]] for b in range(2)], axis=0
            )
            total = total + jnp.dot(lhs, w, preferred_element_type=F32)
        acc[...] = total

    def step(t):
        @pl.when(t < nch)
        def _():
            project(t)

        @pl.when((t >= LAG_ADD) & (t < nch + LAG_ADD))
        def _():
            add_pair(t - LAG_ADD)

        @pl.when((t >= LAG_HID) & (t < nch + LAG_HID))
        def _():
            make_hidden(t - LAG_HID)

        @pl.when((t >= LAG_FWD) & (t < nch + LAG_FWD))
        def _():
            forward(t - LAG_FWD)

        @pl.when(t == LAG_DOWN)
        def _():
            for p in range(pieces):
                weight_copy(2, down_hbm, down_vm, p).wait()

        @pl.when((t >= LAG_DOWN) & (t < nch + LAG_DOWN))
        def _():
            down(t - LAG_DOWN)

    loop(0, nch + LAG_DOWN, step)

    for j in range(sub):
        wide[pl.ds(j, batch, stride=sub), :] = acc[:, j * hd : (j + 1) * hd]

    def narrow(i):
        ret_out[i] = wide[pl.ds(pl.multiple_of(i * tile, tile), tile), :].astype(BF16)

    loop(0, n, narrow)

    def ret_copy(d):
        to = (me + d) % n
        return remote(ret_out.at[to], ret_in.at[me], ret_s.at[d], ret_r.at[d], to)

    def ret_landed(d):
        frm = (me - d + n) % n
        return remote(ret_out.at[0], ret_in.at[frm], ret_s.at[d], ret_r.at[d], frm)

    loop(n // 2, n, lambda d: ret_copy(d).start())
    loop(1, n // 2, lambda d: ret_copy(d).start())
    ret_in[me] = ret_out[me]

    def drain(i):
        pair_copy(i).wait_send()
        for k in range(1, chips):
            chip_copy(i, k).wait_send()
            fwd_copy(i, k).wait_send()
        for k in range(chips):
            hid_copy(i, k).wait_send()

    loop(0, nch, drain)
    loop(1, n, lambda d: x_copy(d).wait_send())
    loop(1, n, lambda d: ret_landed(d).wait_recv())
    for m in range(mdl):
        total = ret_in[m].astype(F32)
        for g in range(1, n // mdl):
            total = total + ret_in[g * mdl + m].astype(F32)
        for r in range(rows):
            at = r * lanes + m * sub
            mixed[at : at + sub, :] = mixed[at : at + sub, :] + total[r * sub : (r + 1) * sub]
    for h in range(lanes):
        out_ref[:, h * hd : (h + 1) * hd] = mixed[pl.ds(h, rows, stride=lanes), :].astype(BF16)
    loop(1, n, lambda d: ret_copy(d).wait_send())


def on_device(
    queries, k_cache, v_cache, lengths, residual_in, norm_gain,
    gate_w, up_w, down_w, block_list, block_count,
):
    n = lax.axis_size("hid")
    rows, heads, hd = queries.shape
    cache = k_cache.shape[1]
    kv = k_cache.shape[2] // hd
    width = residual_in.shape[1]
    _, blocks, ds, bw = gate_w.shape
    mdl = width // ds
    cap = block_list.shape[1]
    cb = 4 if cap % 4 == 0 else 2
    pieces = 7 if blocks % 7 == 0 else 1
    nch = cap // cb
    chips = mdl // 2
    batch = rows * n
    rm = batch // mdl
    sub = ds // hd
    tile = rows * sub
    dims = (n, mdl, rows, heads, hd, kv, cache, width, bw, cap, cb, pieces)
    dma = pltpu.SemaphoreType.DMA
    vmem = pl.BlockSpec(memory_space=pltpu.VMEM)
    smem = pl.BlockSpec(memory_space=pltpu.SMEM)
    hbm = pl.BlockSpec(memory_space=pl.ANY)
    return pl.pallas_call(
        functools.partial(layer_kernel, dims),
        out_shape=jax.ShapeDtypeStruct((rows, width), BF16),
        in_specs=[smem] * 3 + [hbm] * 8,
        out_specs=vmem,
        scratch_shapes=[
            pltpu.VMEM(queries.shape, BF16),
            pltpu.VMEM(residual_in.shape, BF16),
            pltpu.VMEM((width // hd, hd), F32),
            pltpu.VMEM(k_cache.shape, BF16),
            pltpu.VMEM(v_cache.shape, BF16),
            pltpu.VMEM(gate_w.shape[1:], BF16),
            pltpu.VMEM(up_w.shape[1:], BF16),
            pltpu.VMEM(down_w.shape[1:], BF16),
            pltpu.VMEM((rows * (width // hd), hd), F32),
            pltpu.VMEM((mdl, tile, hd), BF16),
            pltpu.VMEM((n, tile, hd), BF16),
            pltpu.VMEM((n * tile, hd), F32),
            pltpu.VMEM((batch, ds), BF16),
            pltpu.VMEM((nch, 2, chips, cb * rm, 2 * bw), BF16),
            pltpu.VMEM((nch, chips, cb * rm, 2 * bw), BF16),
            pltpu.VMEM((nch, chips, cb * rm, 2 * bw), BF16),
            pltpu.VMEM((nch, chips - 1, cb * rm, 2 * bw), BF16),
            pltpu.VMEM((mdl, nch, cb * rm, bw), BF16),
            pltpu.VMEM((batch, ds), F32),
            pltpu.VMEM((n, tile, hd), BF16),
            pltpu.VMEM((n, tile, hd), BF16),
            dma((3,)),
            dma((2, rows)),
            dma((3, pieces)),
            dma((n,)),
            dma((n,)),
            dma((nch,)),
            dma((nch,)),
            dma((nch, chips - 1)),
            dma((nch, chips - 1)),
            dma((nch, chips)),
            dma((nch, chips)),
            dma((nch, chips - 1)),
            dma((nch, chips - 1)),
            dma((n,)),
            dma((n,)),
        ],
        compiler_params=pltpu.CompilerParams(
            collective_id=0, has_side_effects=True, vmem_limit_bytes=63_000_000
        ),
        name="decode_layer",
    )(
        lengths, block_list, block_count, queries, residual_in,
        norm_gain.reshape(width // hd, hd), k_cache, v_cache, gate_w, up_w, down_w,
    )


def solution(mesh):
    in_specs = (
        P(("groups", "hid"), None, None),
        P(("groups", "hid"), None, None),
        P(("groups", "hid"), None, None),
        P(("groups", "hid")),
        P(("groups", "hid"), None),
        P(),
        P("hid", None, None, None),
        P("hid", None, None, None),
        P("hid", None, None, None),
        P("groups", None),
        P("groups"),
    )
    out_specs = P(("groups", "hid"), None)
    return jax.shard_map(
        on_device, mesh=mesh, in_specs=in_specs, out_specs=out_specs, check_vma=False
    )
```

profile of v0, /device:TPU:0, one launch (start us, length us, event | category | flops | bytes accessed | tf_op | source)
XLA Modules:
  0.0 39.8 jit_solution(165401360586669433)
XLA Ops:
  0.0 38.3 %decode_layer.1 = bf16[4,8192]{1,0:T(4,128)(2,1)} custom-call(s32[4]{0:T(128)} %lengths_ref.1, s32[2,28]{1,0:T(2,128)} %list_ref.1, s32[2]{0:T(128)} %count_ref.1, bf16[4,64,128]{2,1,0:T(8,128)(2,1)} %q_hbm.1, bf16[4,8192]{1,0:T(4,128)(2,1)} %res_hbm.1, f32[64,128]{1,0:T(8,128)} %bitcast.1, bf16[4,192,1024]{2,1,0:T(8,128)(2,1)} %k_hbm.1, ...), custom_call_target="tpu_custom_call" | custom-call | tf_op jit(solution)/shard_map/decode_layer/pallas_call | solution.py:419
  38.3 1.5 %copy.13 = bf16[4,8192]{1,0:T(4,128)(2,1)} copy(bf16[4,8192]{1,0:T(4,128)(2,1)} %decode_layer.1) | data formatting | bytes 131072
where the time goes:
time: 40 us; the launch traced here: 39.8 us
  Pallas kernels  38.3 us (96%)
  local copies, waits for them, and re-layouts  1.49 us (4%)
    pallas_call x1, Pallas kernels, on_device(): pl.pallas_call(functools.partial(layer_kernel, dims), out_shape=jax.Shape...  38.3 us
    unnamed x1, local copies, waits for them, and re-layouts  1.49 us

commit v1 on v0

--- a/solution.py
+++ b/solution.py
@@ -12,6 +12,13 @@
 F32 = jnp.float32
 BF16 = jnp.bfloat16
 LAG_ADD, LAG_HID, LAG_FWD, LAG_DOWN = 1, 5, 9, 11
+
+
+def cuts(blocks, cap, cb):
+    first = blocks - cap + cb
+    mid = first + (cap - cb) // cb // 2 * cb
+    edges = sorted({0, first, mid, blocks})
+    return list(zip(edges[:-1], edges[1:]))
 
 
 def layer_kernel(
@@ -33,8 +40,6 @@
     gain_ref,
     k_vm,
     v_vm,
-    gate_vm,
-    up_vm,
     down_vm,
     mixed,
     send_x,
@@ -64,8 +69,13 @@
     fwd_r,
     ret_s,
     ret_r,
+    order_vm,
+    order_sm,
+    order_sem,
+    *wide_w,
 ):
-    n, mdl, rows, heads, hd, kv, cache, width, bw, cap, cb, pieces = dims
+    n, mdl, rows, heads, hd, kv, cache, width, bw, cap, cb, blocks = dims
+    parts_w = cuts(blocks, cap, cb)
     me = lax.axis_index("hid")
     group = me // mdl
     member = me % mdl
@@ -82,7 +92,7 @@
     rm = batch // mdl
     nch = cap // cb
     hpk = heads // kv
-    blk_piece = gate_vm.shape[0] // pieces
+    step_blk = math.gcd(cb, blocks - cap)
 
     small = [
         pltpu.make_async_copy(src, dst, small_sem.at[i])
@@ -100,9 +110,21 @@
         cv.start()
         kv_copies.append((ck, cv))
 
-    def weight_copy(which, hbm, vm, p):
-        span = pl.ds(p * blk_piece, blk_piece)
-        return pltpu.make_async_copy(hbm.at[0, span], vm.at[span], w_sem.at[which, p])
+    def start_weights():
+        for at, (lo, hi) in enumerate(parts_w):
+            for b in range(lo, hi, step_blk):
+                for side_at, src in enumerate((gate_hbm, up_hbm)):
+                    pltpu.make_async_copy(
+                        src.at[0, pl.ds(b, step_blk)],
+                        wide_w[at].at[pl.ds(b - lo, step_blk), side_at],
+                        w_sem.at[at],
+                    ).start()
+        for b in range(0, blocks, step_blk):
+            span = pl.ds(b, step_blk)
+            pltpu.make_async_copy(down_hbm.at[0, span], down_vm.at[span], w_sem.at[3]).start()
+
+    def weights_here(at):
+        pltpu.make_async_copy(wide_w[at], wide_w[at], w_sem.at[at]).wait()
 
     barrier = pltpu.get_barrier_semaphore()
 
@@ -113,6 +135,20 @@
         return carry
 
     lax.fori_loop(1, n, greet, 0)
+
+    side = -(-cap // 8) * 8
+    lane = lax.broadcasted_iota(jnp.int32, (side, 128), 1)
+    sub_at = lax.broadcasted_iota(jnp.int32, (side, 128), 0)
+    listed = jnp.full((side, 128), blocks * 256, jnp.int32)
+    for c in range(cap):
+        listed = jnp.where(lane == c, list_ref[group, c] * 256 + c, listed)
+    down_col = jnp.sum(jnp.where(lane == sub_at, listed, 0), axis=1, keepdims=True)
+    rank = jnp.sum(jnp.where(listed < down_col, 1, 0), axis=1, keepdims=True)
+    order_vm[...] = jnp.sum(
+        jnp.where((rank == lane) & (sub_at < cap), down_col, 0), axis=0, keepdims=True
+    )
+    order_copy = pltpu.make_async_copy(order_vm, order_sm, order_sem)
+    order_copy.start()
 
     for copy in small:
         copy.wait()
@@ -136,9 +172,8 @@
     for ck, cv in kv_copies:
         ck.wait()
         cv.wait()
-    for p in range(pieces):
-        weight_copy(0, gate_hbm, gate_vm, p).start()
-        weight_copy(1, up_hbm, up_vm, p).start()
+    start_weights()
+    order_copy.wait()
     scores = [
         lax.dot_general(
             q_rows[r], k_vm[r], (((1,), (1,)), ((), ())), preferred_element_type=F32
@@ -211,11 +246,6 @@
     for j in range(sub):
         x_vm[:, j * hd : (j + 1) * hd] = wide[pl.ds(j, batch, stride=sub), :].astype(BF16)
 
-    for p in range(pieces):
-        weight_copy(0, gate_hbm, gate_vm, p).wait()
-        weight_copy(1, up_hbm, up_vm, p).wait()
-    for p in range(pieces):
-        weight_copy(2, down_hbm, down_vm, p).start()
 
     def remote(src, dst, ss, rs, to):
         return pltpu.make_async_remote_copy(
@@ -261,13 +291,25 @@
             partner,
         )
 
-    def project(i):
+    def block_of(held, which):
+        def one(at, side_at):
+            lo, hi = parts_w[at]
+            return wide_w[at][jnp.clip(which - lo, 0, hi - lo - 1), side_at]
+
+        both = []
+        for side_at in range(2):
+            w = one(0, side_at)
+            for at in range(1, held):
+                w = jnp.where(which >= parts_w[at][0], one(at, side_at), w)
+            both.append(w)
+        return jnp.concatenate(both, axis=1)
+
+    def project(i, held):
         x = x_vm[...]
         for pair in range(cb // 2):
             got = []
             for b in range(2):
-                which = list_ref[group, i * cb + pair * 2 + b]
-                w = jnp.concatenate([gate_vm[which], up_vm[which]], axis=1)
+                w = block_of(held, order_sm[0, i * cb + pair * 2 + b] // 256)
                 got.append(jnp.dot(x, w, preferred_element_type=F32))
             for m in range(mdl):
                 both = jnp.concatenate([y[m * rm : (m + 1) * rm] for y in got], axis=0)
@@ -292,7 +334,10 @@
             total = total + chip_in[i, k - 1].astype(F32)
         gate, up = total[:, :bw], total[:, bw:]
         row = lax.broadcasted_iota(jnp.int32, gate.shape, 0)
-        active = row < (count_ref[group] - i * cb) * rm
+        active = row < 0
+        for b in range(cb):
+            live = order_sm[0, i * cb + b] % 256 < count_ref[group]
+            active = active | ((row >= b * rm) & (row < jnp.where(live, (b + 1) * rm, 0)))
         hid_all[member, i] = jnp.where(active, jnp.maximum(gate, 0.0) * up, 0.0).astype(BF16)
         for k in range(1, chips):
             hid_copy(i, k).start()
@@ -315,15 +360,25 @@
                 parts.append(jnp.concatenate([two[:rm], two[rm:]], axis=1))
             lhs = jnp.concatenate(parts, axis=0).astype(BF16)
             w = jnp.concatenate(
-                [down_vm[list_ref[group, i * cb + pair * 2 + b]] for b in range(2)], axis=0
+                [down_vm[order_sm[0, i * cb + pair * 2 + b] // 256] for b in range(2)], axis=0
             )
             total = total + jnp.dot(lhs, w, preferred_element_type=F32)
         acc[...] = total
 
     def step(t):
-        @pl.when(t < nch)
-        def _():
-            project(t)
+        first = 0
+        for at in range(len(parts_w)):
+            last = (parts_w[at][1] - (blocks - cap)) // cb
+
+            @pl.when(t == first)
+            def _(at=at):
+                weights_here(at)
+
+            @pl.when((t >= first) & (t < last))
+            def _(at=at):
+                project(t, at + 1)
+
+            first = last
 
         @pl.when((t >= LAG_ADD) & (t < nch + LAG_ADD))
         def _():
@@ -339,8 +394,7 @@
 
         @pl.when(t == LAG_DOWN)
         def _():
-            for p in range(pieces):
-                weight_copy(2, down_hbm, down_vm, p).wait()
+            pltpu.make_async_copy(down_vm, down_vm, w_sem.at[3]).wait()
 
         @pl.when((t >= LAG_DOWN) & (t < nch + LAG_DOWN))
         def _():
@@ -404,21 +458,20 @@
     mdl = width // ds
     cap = block_list.shape[1]
     cb = 4 if cap % 4 == 0 else 2
-    pieces = 7 if blocks % 7 == 0 else 1
     nch = cap // cb
     chips = mdl // 2
     batch = rows * n
     rm = batch // mdl
     sub = ds // hd
     tile = rows * sub
-    dims = (n, mdl, rows, heads, hd, kv, cache, width, bw, cap, cb, pieces)
+    dims = (n, mdl, rows, heads, hd, kv, cache, width, bw, cap, cb, blocks)
     dma = pltpu.SemaphoreType.DMA
     vmem = pl.BlockSpec(memory_space=pltpu.VMEM)
     smem = pl.BlockSpec(memory_space=pltpu.SMEM)
     hbm = pl.BlockSpec(memory_space=pl.ANY)
     return pl.pallas_call(
         functools.partial(layer_kernel, dims),
-        out_shape=jax.ShapeDtypeStruct((rows, width), BF16),
+        out_shape=pltpu.VMEM((rows, width), BF16),
         in_specs=[smem] * 3 + [hbm] * 8,
         out_specs=vmem,
         scratch_shapes=[
@@ -427,8 +480,6 @@
             pltpu.VMEM((width // hd, hd), F32),
             pltpu.VMEM(k_cache.shape, BF16),
             pltpu.VMEM(v_cache.shape, BF16),
-            pltpu.VMEM(gate_w.shape[1:], BF16),
-            pltpu.VMEM(up_w.shape[1:], BF16),
             pltpu.VMEM(down_w.shape[1:], BF16),
             pltpu.VMEM((rows * (width // hd), hd), F32),
             pltpu.VMEM((mdl, tile, hd), BF16),
@@ -445,7 +496,7 @@
             pltpu.VMEM((n, tile, hd), BF16),
             dma((3,)),
             dma((2, rows)),
-            dma((3, pieces)),
+            dma((4,)),
             dma((n,)),
             dma((n,)),
             dma((nch,)),
@@ -458,7 +509,11 @@
             dma((nch, chips - 1)),
             dma((n,)),
             dma((n,)),
-        ],
+            pltpu.VMEM((1, 128), jnp.int32),
+            pltpu.SMEM((1, 128), jnp.int32),
+            dma(()),
+        ]
+        + [pltpu.VMEM((hi - lo, 2, ds, bw), BF16) for lo, hi in cuts(blocks, cap, cb)],
         compiler_params=pltpu.CompilerParams(
             collective_id=0, has_side_effects=True, vmem_limit_bytes=63_000_000
         ),

time: 40 us -> 36.7 us (0.918)
  Pallas kernels: 38.3 us -> 35.9 us
  local copies, waits for them, and re-layouts: 1.49 us -> 0.63 us
    pallas_call x1, Pallas kernels: 38.3 us -> 35.9 us  [on_device(): pl.pallas_call(functools.partial(layer_kernel, dims), out_shape=pltpu.VME...]
    unnamed x1, local copies, waits for them, and re-layouts: 1.49 us -> 0.63 us
where the time goes in v1:
time: 36.7 us; the launch traced here: 36.5 us
  Pallas kernels  35.9 us (98%)
  local copies, waits for them, and re-layouts  0.63 us (2%)
    pallas_call x1, Pallas kernels, on_device(): pl.pallas_call(functools.partial(layer_kernel, dims), out_shape=pltpu.VME...  35.9 us

profile of v1, /device:TPU:0, one launch (start us, length us, event | category | flops | bytes accessed | tf_op | source)
XLA Modules:
  0.0 36.5 jit_solution(4928331727563578757)
XLA Ops:
  0.0 35.9 %decode_layer.1 = bf16[4,8192]{1,0:T(4,128)(2,1)S(1)} custom-call(s32[4]{0:T(128)} %lengths_ref.1, s32[2,28]{1,0:T(2,128)} %list_ref.1, s32[2]{0:T(128)} %count_ref.1, bf16[4,64,128]{2,1,0:T(8,128)(2,1)} %q_hbm.1, bf16[4,8192]{1,0:T(4,128)(2,1)} %res_hbm.1, f32[64,128]{1,0:T(8,128)} %bitcast.1, bf16[4,192,1024]{2,1,0:T(8,128)(2,1)} %k_hbm.1, ...), custom_call_target="tpu_custom_call" | custom-call | tf_op jit(solution)/shard_map/decode_layer/pallas_call | solution.py:472
  35.9 0.6 %copy.13 = bf16[4,8192]{1,0:T(4,128)(2,1)} copy(bf16[4,8192]{1,0:T(4,128)(2,1)S(1)} %decode_layer.1) | data formatting | bytes 131072

commit v2 on v0

v2 whole, which is shorter than its diff:
```python
import functools
import math

import jax
import jax.numpy as jnp
from jax import lax
from jax.experimental import pallas as pl
from jax.experimental.pallas import tpu as pltpu
from jax.sharding import PartitionSpec as P

MESH = pl.DeviceIdType.MESH
F32 = jnp.float32
BF16 = jnp.bfloat16
FAR, NEAR = 0, 1
KV_FIRST = 0
GATE_SETS, NEAR_SETS = (2, 4), (4,)
T_GATE_ADD = (-2, 2.0)
T_FAR_ADD = (4.5,)
T_NEAR_ADD = (11.6, 1)
T_FAR_HID = (20,)
T_NEAR_HID = (28.5, 0.1)
T_FAR_FWD = (30,)
T_FAR_DOWN = (34.5,)
T_NEAR_FWD = (37.9, 2)


def cut(count, edges):
    edges = [0, *(e for e in edges if e < count), count]
    return list(zip(edges[:-1], edges[1:]))


def layer_kernel(
    dims,
    lengths_ref,
    list_ref,
    count_ref,
    q_hbm,
    res_hbm,
    gain_hbm,
    k_hbm,
    v_hbm,
    gate_hbm,
    up_hbm,
    down_hbm,
    out_ref,
    q_ref,
    res_ref,
    gain_ref,
    kv_vm,
    gate_vm,
    up_vm,
    down_vm,
    mixed,
    send_x,
    arrived,
    wide,
    x_vm,
    pair_out,
    pair_in,
    chip_out,
    chip_in,
    hid_all,
    acc,
    ret_out,
    ret_in,
    small_sem,
    kv_sem,
    w_sem,
    x_s,
    x_r,
    pair_s,
    pair_r,
    chip_s,
    chip_r,
    hid_s,
    hid_r,
    fwd_s,
    fwd_r,
    ret_s,
    ret_r,
):
    n, mdl, rows, heads, hd, kv, cache, width, bw, cap, cb, blocks, groups = dims
    me = lax.axis_index("hid")
    group = me // mdl
    member = me % mdl
    base = group * mdl
    core = member % 2
    chip = member // 2
    chips = mdl // 2
    partner = base + chip * 2 + (1 - core)
    ds = width // mdl
    sub = ds // hd
    lanes = width // hd
    tile = rows * sub
    batch = rows * n
    nch = cap // cb
    hpk = heads // kv
    far_n = n - mdl
    part_rows = (rows * far_n, rows * mdl)
    part_at = (0, rows * far_n)
    rp = tuple(v // chips for v in part_rows)
    span = (pl.ds(0, 2 * rp[0]), pl.ds(2 * rp[0], 2 * rp[1]))
    step_blk = math.gcd(8, blocks)

    small = [
        pltpu.make_async_copy(src, dst, small_sem.at[i])
        for i, (src, dst) in enumerate(
            ((res_hbm, res_ref), (q_hbm, q_ref), (gain_hbm, gain_ref))
        )
    ]
    for copy in small:
        copy.start()
    for r in range(rows):
        pltpu.make_async_copy(k_hbm.at[r], kv_vm.at[r, 0], kv_sem.at[r]).start()
        pltpu.make_async_copy(v_hbm.at[r], kv_vm.at[r, 1], kv_sem.at[r]).start()

    def start_weights():
        for which, (src, vm) in enumerate(
            ((gate_hbm, gate_vm), (up_hbm, up_vm), (down_hbm, down_vm))
        ):
            for b in range(0, blocks, step_blk):
                at = pl.ds(b, step_blk)
                pltpu.make_async_copy(src.at[0, at], vm.at[at], w_sem.at[which]).start()

    def weights_here(which, vm):
        pltpu.make_async_copy(vm, vm, w_sem.at[which]).wait()

    barrier = pltpu.get_barrier_semaphore()

    def greet(d, carry):
        pl.semaphore_signal(
            barrier, inc=1, device_id={"hid": (me + d) % n}, device_id_type=MESH
        )
        return carry

    lax.fori_loop(1, n, greet, 0)

    for copy in small:
        copy.wait()
    for h in range(lanes):
        mixed[pl.ds(h, rows, stride=lanes), :] = res_ref[:, h * hd : (h + 1) * hd].astype(F32)

    slot = lax.broadcasted_iota(jnp.int32, (heads, cache), 1)
    q_rows = []
    for r in range(rows):
        q = q_ref[r].astype(F32)
        cols = []
        for k in range(kv):
            parts = []
            if k > 0:
                parts.append(jnp.zeros((k * hpk, hd), F32))
            parts.append(q[k * hpk : (k + 1) * hpk])
            if k < kv - 1:
                parts.append(jnp.zeros(((kv - 1 - k) * hpk, hd), F32))
            cols.append(jnp.concatenate(parts, axis=0).astype(BF16))
        q_rows.append(jnp.concatenate(cols, axis=1))
    for r in range(rows):
        if r == KV_FIRST:
            start_weights()
        pltpu.make_async_copy(kv_vm.at[r], kv_vm.at[r], kv_sem.at[r]).wait()
    scores = [
        lax.dot_general(
            q_rows[r], kv_vm[r, 0], (((1,), (1,)), ((), ())), preferred_element_type=F32
        ) * (1.0 / math.sqrt(hd))
        for r in range(rows)
    ]
    valid = [slot < lengths_ref[r] for r in range(rows)]
    scores = [jnp.where(valid[r], scores[r], -1e30) for r in range(rows)]
    tops = [jnp.max(v, axis=1, keepdims=True) for v in scores]
    terms = [jnp.where(valid[r], jnp.exp(scores[r] - tops[r]), 0.0) for r in range(rows)]
    sums = [jnp.sum(v, axis=1, keepdims=True) for v in terms]
    probs = [(terms[r] / sums[r]).astype(BF16) for r in range(rows)]
    mixed_rows = []
    for r in range(rows):
        wide_att = jnp.dot(probs[r], kv_vm[r, 1], preferred_element_type=F32)
        att = jnp.concatenate(
            [wide_att[k * hpk : (k + 1) * hpk, k * hd : (k + 1) * hd] for k in range(kv)],
            axis=0,
        )
        mixed_rows.append(mixed[r * lanes : (r + 1) * lanes, :] + att)
    normed = []
    for r in range(rows):
        row = mixed_rows[r]
        mixed[r * lanes : (r + 1) * lanes, :] = row
        mean_sq = (
            jnp.sum(jnp.sum(row * row, axis=1, keepdims=True), axis=0, keepdims=True) / width
        )
        normed.append(row * lax.rsqrt(mean_sq + 1e-05) * gain_ref[...])
    for m in range(mdl):
        piece = jnp.concatenate([v[m * sub : (m + 1) * sub] for v in normed], axis=0)
        send_x[m] = piece.astype(BF16)

    pl.semaphore_wait(barrier, n - 1)

    def remote(src, dst, ss, rs, to):
        return pltpu.make_async_remote_copy(
            src_ref=src, dst_ref=dst, send_sem=ss, recv_sem=rs,
            device_id={"hid": to}, device_id_type=MESH,
        )

    def landed(ref, sem):
        remote(ref, ref, x_s, sem, partner).wait_recv()

    def sent(ref, sem):
        remote(ref, ref, sem, ret_r.at[0], partner).wait_send()

    def loop(lo, hi, f):
        def body(i, carry):
            f(i)
            return carry

        lax.fori_loop(lo, hi, body, 0)

    def far_dev(k):
        return (group + 1 + k // mdl) % groups * mdl + (member + k % mdl) % mdl

    def near_dev(d):
        return base + (member + d) % mdl

    def x_copy(to, sem):
        return remote(send_x.at[to % mdl], arrived.at[me], x_s, sem, to)

    loop(0, far_n, lambda k: x_copy(far_dev(k), x_r.at[FAR]).start())
    loop(1, mdl, lambda d: x_copy(near_dev(d), x_r.at[NEAR]).start())
    arrived[me] = send_x[member]
    acc[...] = jnp.zeros_like(acc)

    def widen(at, src):
        wide[pl.ds(pl.multiple_of(at * tile, tile), tile), :] = arrived[src].astype(F32)

    landed(arrived.at[pl.ds(0, mdl - 1)], x_r.at[NEAR])
    loop(0, mdl, lambda m: widen(far_n + m, base + m))
    landed(arrived.at[pl.ds(0, far_n)], x_r.at[FAR])
    loop(0, far_n, lambda k: widen(k, (base + mdl + k) % n))
    for j in range(sub):
        x_vm[:, j * hd : (j + 1) * hd] = wide[pl.ds(j, batch, stride=sub), :].astype(BF16)
    weights_here(0, gate_vm)

    def pair_cols(vm, i, c):
        at = i * cb + c * 2
        return jnp.concatenate([vm[list_ref[group, at + b]] for b in range(2)], axis=1)

    def pack(y, s, i, c):
        for q in range(chips):
            for p in range(2):
                lo = part_at[p] + q * rp[p]
                y_q = y[lo : lo + rp[p]]
                pair_out[s, i, c, q, span[p], :] = jnp.concatenate(
                    [y_q[:, :bw], y_q[:, bw:]], axis=0
                ).astype(BF16)

    def gate_chunk(i):
        x = x_vm[...]
        for c in range(2):
            y = jnp.dot(x, pair_cols(gate_vm, i, c), preferred_element_type=F32)
            pack(y, 0, i, c)

    def up_chunk(i):
        x = x_vm[...]
        for c in range(2):
            y = jnp.dot(x, pair_cols(up_vm, i, c), preferred_element_type=F32)
            pack(y, 1, i, c)

    both = pl.ds(0, 2 * (rp[0] + rp[1]))

    def pair_copy(s, at, row, sem):
        return remote(
            pair_out.at[s, at, 1 - core, :, row], pair_in.at[s, at, :, row], pair_s, sem, partner
        )

    def add_pair(s, at, row):
        total = pair_out[s, at, core, :, row].astype(F32) + pair_in[s, at, :, row].astype(F32)
        chip_out[s, at, :, row] = total.astype(BF16)

    def chip_start(s, at, row, sem):
        for k in range(1, chips):
            to = (chip + k) % chips
            remote(
                chip_out.at[s, at, to, row], chip_in.at[s, at, k - 1, row], chip_s, sem,
                base + to * 2 + core,
            ).start()

    def total_of(s, i, row):
        total = chip_out[s, i, chip, row].astype(F32)
        for k in range(1, chips):
            total = total + chip_in[s, i, k - 1, row].astype(F32)
        return total

    def make_hidden(i, p):
        gate, up = total_of(0, i, span[p]), total_of(1, i, span[p])
        row = lax.broadcasted_iota(jnp.int32, gate.shape, 0)
        active = row < (count_ref[group] - (i * cb + core * 2)) * rp[p]
        hid_all[i, core, chip, span[p], :] = jnp.where(
            active, jnp.maximum(gate, 0.0) * up, 0.0
        ).astype(BF16)

    def hid_start(at, row, sem):
        for k in range(1, chips):
            to = (chip + k) % chips
            ref = hid_all.at[at, core, chip, row]
            remote(ref, ref, hid_s, sem, base + to * 2 + core).start()

    def hid_landed(at, row, sem):
        landed(hid_all.at[at, 0, pl.ds(0, chips - 1), row], sem)

    def fwd_copy(at, row, sem):
        ref = hid_all.at[at, core, :, row]
        return remote(ref, ref, fwd_s, sem, partner)

    def down(i, p):
        total = acc[pl.ds(part_at[p], part_rows[p]), :]
        for c in range(2):
            parts = []
            for q in range(chips):
                two = hid_all[i, c, q, span[p], :].astype(F32)
                parts.append(jnp.concatenate([two[: rp[p]], two[rp[p] :]], axis=1))
            lhs = jnp.concatenate(parts, axis=0).astype(BF16)
            w = jnp.concatenate(
                [down_vm[list_ref[group, i * cb + c * 2 + b]] for b in range(2)], axis=0
            )
            total = total + jnp.dot(lhs, w, preferred_element_type=F32)
        acc[pl.ds(part_at[p], part_rows[p]), :] = total

    gate_sets, near_sets = cut(nch, GATE_SETS), cut(nch, NEAR_SETS)
    G0, N0 = 0, len(gate_sets)
    C0 = N0 + len(near_sets)

    def ats(lo_hi):
        lo, hi = lo_hi
        return pl.ds(lo, hi - lo)

    def one(i):
        return pl.ds(i, 1)

    def gate_set(g):
        for i in range(*gate_sets[g]):
            gate_chunk(i)
        pair_copy(0, ats(gate_sets[g]), both, pair_r.at[G0 + g]).start()

    def gate_add(g):
        landed(pair_in.at[0, ats(gate_sets[g]), :, both], pair_r.at[G0 + g])
        loop(*gate_sets[g], lambda i: add_pair(0, i, both))
        chip_start(0, ats(gate_sets[g]), both, chip_r.at[G0 + g])

    def gate_land(g):
        landed(chip_in.at[0, ats(gate_sets[g]), :, both], chip_r.at[G0 + g])

    def far_up(i):
        up_chunk(i)
        pair_copy(1, one(i), span[FAR], pair_r.at[C0 + i]).start()

    def far_add(i):
        landed(pair_in.at[1, one(i), :, span[FAR]], pair_r.at[C0 + i])
        add_pair(1, i, span[FAR])
        chip_start(1, one(i), span[FAR], chip_r.at[C0 + i])

    def near_pair(g):
        pair_copy(1, ats(near_sets[g]), span[NEAR], pair_r.at[N0 + g]).start()

    def far_hidden(i):
        landed(chip_in.at[1, one(i), :, span[FAR]], chip_r.at[C0 + i])
        make_hidden(i, FAR)
        hid_start(one(i), span[FAR], hid_r.at[C0 + i])

    def far_forward(i):
        hid_landed(one(i), span[FAR], hid_r.at[C0 + i])
        fwd_copy(one(i), span[FAR], fwd_r.at[C0 + i]).start()

    def far_down(i):
        landed(hid_all.at[one(i), 0, :, span[FAR]], fwd_r.at[C0 + i])
        down(i, FAR)

    def near_add(g):
        landed(pair_in.at[1, ats(near_sets[g]), :, span[NEAR]], pair_r.at[N0 + g])
        loop(*near_sets[g], lambda i: add_pair(1, i, span[NEAR]))
        chip_start(1, ats(near_sets[g]), span[NEAR], chip_r.at[N0 + g])

    def near_hidden(g):
        landed(chip_in.at[1, ats(near_sets[g]), :, span[NEAR]], chip_r.at[N0 + g])
        loop(*near_sets[g], lambda i: make_hidden(i, NEAR))
        hid_start(ats(near_sets[g]), span[NEAR], hid_r.at[N0 + g])

    def near_forward(g):
        hid_landed(ats(near_sets[g]), span[NEAR], hid_r.at[N0 + g])
        fwd_copy(ats(near_sets[g]), span[NEAR], fwd_r.at[N0 + g]).start()

    def near_down(g):
        landed(hid_all.at[ats(near_sets[g]), 0, :, span[NEAR]], fwd_r.at[N0 + g])
        loop(*near_sets[g], lambda i: down(i, NEAR))

    def down_here(_):
        weights_here(2, down_vm)

    def narrow(k):
        ret_out[k] = wide[pl.ds(pl.multiple_of(k * tile, tile), tile), :].astype(BF16)

    def spread(p):
        for j in range(sub):
            wide[pl.ds(part_at[p] * sub + j, part_rows[p], stride=sub), :] = acc[
                pl.ds(part_at[p], part_rows[p]), j * hd : (j + 1) * hd
            ]

    def far_slot(k):
        to = far_dev(k)
        return (to - base - mdl + n) % n

    def far_return(_):
        spread(FAR)
        loop(0, far_n, narrow)
        loop(
            0,
            far_n,
            lambda k: remote(
                ret_out.at[far_slot(k)], ret_in.at[me], ret_s, ret_r.at[FAR], far_dev(k)
            ).start(),
        )

    def near_return(_):
        spread(NEAR)
        loop(far_n, n, narrow)
        loop(
            1,
            mdl,
            lambda d: remote(
                ret_out.at[far_n + (member + d) % mdl], ret_in.at[me], ret_s,
                ret_r.at[NEAR], near_dev(d),
            ).start(),
        )
        ret_in[me] = ret_out[far_n + member]

    ops = []

    def put(f, count, first, step=1.0):
        for i in range(count):
            ops.append((first + i * step, len(ops), f, i))

    ng, nn = len(gate_sets), len(near_sets)
    put(gate_set, ng, -20)
    put(gate_add, ng, *T_GATE_ADD)
    put(lambda _: weights_here(1, up_vm), 1, -0.5)
    put(far_up, nch, 0)
    for g, (lo, hi) in enumerate(near_sets):
        ops.append((hi - 0.9, len(ops), near_pair, g))
    put(far_add, nch, *T_FAR_ADD)
    put(near_add, nn, *T_NEAR_ADD)
    put(gate_land, ng, T_FAR_HID[0] - 0.5, 0.01)
    put(far_hidden, nch, *T_FAR_HID)
    put(near_hidden, nn, *T_NEAR_HID)
    put(far_forward, nch, *T_FAR_FWD)
    put(down_here, 1, T_FAR_DOWN[0] - 0.05)
    put(far_down, nch, *T_FAR_DOWN)
    end = max(t for t, *_ in ops)
    put(far_return, 1, end + 1)
    put(near_forward, nn, *T_NEAR_FWD)
    put(near_down, nn, end + 20)
    put(near_return, 1, end + 30)
    for _, _, f, i in sorted(ops, key=lambda v: v[:2]):
        f(i)

    sent(arrived.at[pl.ds(0, n - 1)], x_s)
    sent(pair_in, pair_s)
    sent(chip_in, chip_s)
    sent(hid_all.at[:, 0, pl.ds(0, chips - 1)], hid_s)
    sent(hid_all.at[:, 0], fwd_s)
    landed(ret_in.at[pl.ds(0, mdl - 1)], ret_r.at[NEAR])
    landed(ret_in.at[pl.ds(0, far_n)], ret_r.at[FAR])
    for m in range(mdl):
        total = ret_in[m].astype(F32)
        for g in range(1, groups):
            total = total + ret_in[g * mdl + m].astype(F32)
        for r in range(rows):
            at = r * lanes + m * sub
            mixed[at : at + sub, :] = mixed[at : at + sub, :] + total[r * sub : (r + 1) * sub]
    for h in range(lanes):
        out_ref[:, h * hd : (h + 1) * hd] = mixed[pl.ds(h, rows, stride=lanes), :].astype(BF16)
    sent(ret_in.at[pl.ds(0, n - 1)], ret_s)


def on_device(
    queries, k_cache, v_cache, lengths, residual_in, norm_gain,
    gate_w, up_w, down_w, block_list, block_count,
):
    n = lax.axis_size("hid")
    rows, heads, hd = queries.shape
    cache = k_cache.shape[1]
    kv = k_cache.shape[2] // hd
    width = residual_in.shape[1]
    _, blocks, ds, bw = gate_w.shape
    mdl = width // ds
    cap = block_list.shape[1]
    cb = 4
    nch = cap // cb
    chips = mdl // 2
    batch = rows * n
    sub = ds // hd
    tile = rows * sub
    groups = n // mdl
    piece = 2 * batch // chips
    marks = len(cut(nch, GATE_SETS)) + len(cut(nch, NEAR_SETS)) + nch
    dims = (n, mdl, rows, heads, hd, kv, cache, width, bw, cap, cb, blocks, groups)
    dma = pltpu.SemaphoreType.DMA
    vmem = pl.BlockSpec(memory_space=pltpu.VMEM)
    smem = pl.BlockSpec(memory_space=pltpu.SMEM)
    hbm = pl.BlockSpec(memory_space=pl.ANY)
    return pl.pallas_call(
        functools.partial(layer_kernel, dims),
        out_shape=pltpu.VMEM((rows, width), BF16),
        in_specs=[smem] * 3 + [hbm] * 8,
        out_specs=vmem,
        scratch_shapes=[
            pltpu.VMEM(queries.shape, BF16),
            pltpu.VMEM(residual_in.shape, BF16),
            pltpu.VMEM((width // hd, hd), F32),
            pltpu.VMEM((rows, 2, cache, kv * hd), BF16),
            pltpu.VMEM(gate_w.shape[1:], BF16),
            pltpu.VMEM(up_w.shape[1:], BF16),
            pltpu.VMEM(down_w.shape[1:], BF16),
            pltpu.VMEM((rows * (width // hd), hd), F32),
            pltpu.VMEM((mdl, tile, hd), BF16),
            pltpu.VMEM((n, tile, hd), BF16),
            pltpu.VMEM((n * tile, hd), F32),
            pltpu.VMEM((batch, ds), BF16),
            pltpu.VMEM((2, nch, 2, chips, piece, bw), BF16),
            pltpu.VMEM((2, nch, chips, piece, bw), BF16),
            pltpu.VMEM((2, nch, chips, piece, bw), BF16),
            pltpu.VMEM((2, nch, chips - 1, piece, bw), BF16),
            pltpu.VMEM((nch, 2, chips, piece, bw), BF16),
            pltpu.VMEM((batch, ds), F32),
            pltpu.VMEM((n, tile, hd), BF16),
            pltpu.VMEM((n, tile, hd), BF16),
            dma((3,)),
            dma((rows,)),
            dma((3,)),
            dma(()),
            dma((2,)),
            dma(()),
            dma((marks,)),
            dma(()),
            dma((marks,)),
            dma(()),
            dma((marks,)),
            dma(()),
            dma((marks,)),
            dma(()),
            dma((2,)),
        ],
        compiler_params=pltpu.CompilerParams(
            collective_id=0, has_side_effects=True, vmem_limit_bytes=63_000_000
        ),
        name="decode_layer",
    )(
        lengths, block_list, block_count, queries, residual_in,
        norm_gain.reshape(width // hd, hd), k_cache, v_cache, gate_w, up_w, down_w,
    )


def solution(mesh):
    in_specs = (
        P(("groups", "hid"), None, None),
        P(("groups", "hid"), None, None),
        P(("groups", "hid"), None, None),
        P(("groups", "hid")),
        P(("groups", "hid"), None),
        P(),
        P("hid", None, None, None),
        P("hid", None, None, None),
        P("hid", None, None, None),
        P("groups", None),
        P("groups"),
    )
    out_specs = P(("groups", "hid"), None)
    return jax.shard_map(
        on_device, mesh=mesh, in_specs=in_specs, out_specs=out_specs, check_vma=False
    )
```

time: 40 us -> 32.9 us (0.82)
  Pallas kernels: 38.3 us -> 32.1 us
  local copies, waits for them, and re-layouts: 1.49 us -> 0.63 us
    pallas_call x1, Pallas kernels: 38.3 us -> 32.1 us  [on_device(): pl.pallas_call(functools.partial(layer_kernel, dims), out_shape=pltpu.VME...]
    unnamed x1, local copies, waits for them, and re-layouts: 1.49 us -> 0.63 us
where the time goes in v2:
time: 32.9 us; the launch traced here: 32.8 us
  Pallas kernels  32.1 us (98%)
  local copies, waits for them, and re-layouts  0.63 us (2%)
    pallas_call x1, Pallas kernels, on_device(): pl.pallas_call(functools.partial(layer_kernel, dims), out_shape=pltpu.VME...  32.1 us

profile of v2, /device:TPU:0, one launch (start us, length us, event | category | flops | bytes accessed | tf_op | source)
XLA Modules:
  0.0 32.8 jit_solution(12324814718207168903)
XLA Ops:
  0.0 32.1 %decode_layer.1 = bf16[4,8192]{1,0:T(4,128)(2,1)S(1)} custom-call(s32[4]{0:T(128)} %lengths_ref.1, s32[2,28]{1,0:T(2,128)} %list_ref.1, s32[2]{0:T(128)} %count_ref.1, bf16[4,64,128]{2,1,0:T(8,128)(2,1)} %q_hbm.1, bf16[4,8192]{1,0:T(4,128)(2,1)} %res_hbm.1, f32[64,128]{1,0:T(8,128)} %bitcast.1, bf16[4,192,1024]{2,1,0:T(8,128)(2,1)} %k_hbm.1, ...), custom_call_target="tpu_custom_call" | custom-call | tf_op jit(solution)/shard_map/decode_layer/pallas_call | solution.py:505
  32.1 0.6 %copy.13 = bf16[4,8192]{1,0:T(4,128)(2,1)} copy(bf16[4,8192]{1,0:T(4,128)(2,1)S(1)} %decode_layer.1) | data formatting | bytes 131072

commit v3 on v2

--- a/solution.py
+++ b/solution.py
@@ -13,14 +13,21 @@
 BF16 = jnp.bfloat16
 FAR, NEAR = 0, 1
 KV_FIRST = 0
-GATE_SETS, NEAR_SETS = (2, 4), (4,)
-T_GATE_ADD = (-2, 2.0)
-T_FAR_ADD = (4.5,)
+EARLY = 1
+DOWN_AT = 1
+FARTHEST = True
+GATE_WHOLE = True
+GATE_SETS = (2, 4)
+NEAR_SETS = (4,)
+FAR_SETS = (1, 2, 3, 4, 5, 6)
+DIRECT = ()
+T_GATE_ADD = (-2, 1.2)
+T_FAR_ADD = (4.5, 1)
 T_NEAR_ADD = (11.6, 1)
-T_FAR_HID = (20,)
+T_FAR_HID = (20, 1)
 T_NEAR_HID = (28.5, 0.1)
-T_FAR_FWD = (30,)
-T_FAR_DOWN = (34.5,)
+T_FAR_FWD = (30, 1)
+T_FAR_DOWN = (34.5, 1)
 T_NEAR_FWD = (37.9, 2)
 
 
@@ -31,9 +38,9 @@
 
 def layer_kernel(
     dims,
-    lengths_ref,
-    list_ref,
-    count_ref,
+    lengths_hbm,
+    list_hbm,
+    count_hbm,
     q_hbm,
     res_hbm,
     gain_hbm,
@@ -78,6 +85,10 @@
     fwd_r,
     ret_s,
     ret_r,
+    lengths_ref,
+    list_ref,
+    count_ref,
+    tab_sem,
 ):
     n, mdl, rows, heads, hd, kv, cache, width, bw, cap, cb, blocks, groups = dims
     me = lax.axis_index("hid")
@@ -94,6 +105,7 @@
     tile = rows * sub
     batch = rows * n
     nch = cap // cb
+    quad = mdl // 2
     hpk = heads // kv
     far_n = n - mdl
     part_rows = (rows * far_n, rows * mdl)
@@ -114,17 +126,26 @@
         pltpu.make_async_copy(k_hbm.at[r], kv_vm.at[r, 0], kv_sem.at[r]).start()
         pltpu.make_async_copy(v_hbm.at[r], kv_vm.at[r, 1], kv_sem.at[r]).start()
 
-    def start_weights():
-        for which, (src, vm) in enumerate(
-            ((gate_hbm, gate_vm), (up_hbm, up_vm), (down_hbm, down_vm))
-        ):
-            for b in range(0, blocks, step_blk):
-                at = pl.ds(b, step_blk)
-                pltpu.make_async_copy(src.at[0, at], vm.at[at], w_sem.at[which]).start()
+    tables = [
+        pltpu.make_async_copy(src, dst, tab_sem.at[i])
+        for i, (src, dst) in enumerate(
+            ((lengths_hbm, lengths_ref), (list_hbm, list_ref), (count_hbm, count_ref))
+        )
+    ]
+    for copy in tables:
+        copy.start()
+
+    def start_weights(which, lo, hi):
+        src, vm = ((gate_hbm, gate_vm), (up_hbm, up_vm), (down_hbm, down_vm))[which]
+        for b in range(lo, hi, step_blk):
+            at = pl.ds(b, step_blk)
+            pltpu.make_async_copy(src.at[0, at], vm.at[at], w_sem.at[which]).start()
 
     def weights_here(which, vm):
         pltpu.make_async_copy(vm, vm, w_sem.at[which]).wait()
 
+    early = min(EARLY * step_blk, blocks)
+    start_weights(0, 0, early)
     barrier = pltpu.get_barrier_semaphore()
 
     def greet(d, carry):
@@ -136,6 +157,8 @@
     lax.fori_loop(1, n, greet, 0)
 
     for copy in small:
+        copy.wait()
+    for copy in tables:
         copy.wait()
     for h in range(lanes):
         mixed[pl.ds(h, rows, stride=lanes), :] = res_ref[:, h * hd : (h + 1) * hd].astype(F32)
@@ -156,7 +179,10 @@
         q_rows.append(jnp.concatenate(cols, axis=1))
     for r in range(rows):
         if r == KV_FIRST:
-            start_weights()
+            start_weights(0, early, blocks)
+            start_weights(1, 0, blocks)
+            if DOWN_AT == 0:
+                start_weights(2, 0, blocks)
         pltpu.make_async_copy(kv_vm.at[r], kv_vm.at[r], kv_sem.at[r]).wait()
     scores = [
         lax.dot_general(
@@ -212,7 +238,9 @@
         lax.fori_loop(lo, hi, body, 0)
 
     def far_dev(k):
-        return (group + 1 + k // mdl) % groups * mdl + (member + k % mdl) % mdl
+        ahead, way = k // mdl, k % mdl
+        turn = (way // quad + 1 + group) % 2 * quad + (member + way) % quad
+        return (group + 1 + ahead) % groups * mdl + (turn if FARTHEST else (member + way) % mdl)
 
     def near_dev(d):
         return base + (member + d) % mdl
@@ -228,9 +256,13 @@
     def widen(at, src):
         wide[pl.ds(pl.multiple_of(at * tile, tile), tile), :] = arrived[src].astype(F32)
 
+    if DOWN_AT == 1:
+        start_weights(2, 0, blocks)
     landed(arrived.at[pl.ds(0, mdl - 1)], x_r.at[NEAR])
     loop(0, mdl, lambda m: widen(far_n + m, base + m))
     landed(arrived.at[pl.ds(0, far_n)], x_r.at[FAR])
+    if DOWN_AT == 2:
+        start_weights(2, 0, blocks)
     loop(0, far_n, lambda k: widen(k, (base + mdl + k) % n))
     for j in range(sub):
         x_vm[:, j * hd : (j + 1) * hd] = wide[pl.ds(j, batch, stride=sub), :].astype(BF16)
@@ -299,6 +331,12 @@
             to = (chip + k) % chips
             ref = hid_all.at[at, core, chip, row]
             remote(ref, ref, hid_s, sem, base + to * 2 + core).start()
+
+    def cross_start(at, row, sem):
+        for k in range(chips):
+            to = (chip + (k + 1) % chips) % chips
+            ref = hid_all.at[at, core, chip, row]
+            remote(ref, ref, fwd_s, sem, base + to * 2 + (1 - core)).start()
 
     def hid_landed(at, row, sem):
         landed(hid_all.at[at, 0, pl.ds(0, chips - 1), row], sem)
@@ -323,14 +361,12 @@
 
     gate_sets, near_sets = cut(nch, GATE_SETS), cut(nch, NEAR_SETS)
     G0, N0 = 0, len(gate_sets)
+    far_sets = cut(nch, FAR_SETS)
     C0 = N0 + len(near_sets)
 
     def ats(lo_hi):
         lo, hi = lo_hi
         return pl.ds(lo, hi - lo)
-
-    def one(i):
-        return pl.ds(i, 1)
 
     def gate_set(g):
         for i in range(*gate_sets[g]):
@@ -340,35 +376,47 @@
     def gate_add(g):
         landed(pair_in.at[0, ats(gate_sets[g]), :, both], pair_r.at[G0 + g])
         loop(*gate_sets[g], lambda i: add_pair(0, i, both))
-        chip_start(0, ats(gate_sets[g]), both, chip_r.at[G0 + g])
+        if GATE_WHOLE:
+            chip_start(0, ats(gate_sets[g]), both, chip_r.at[G0 + g])
+        else:
+            chip_start(0, ats(gate_sets[g]), span[FAR], chip_r.at[G0 + g])
+            chip_start(0, ats(gate_sets[g]), span[NEAR], chip_r.at[G0 + g])
 
     def gate_land(g):
         landed(chip_in.at[0, ats(gate_sets[g]), :, both], chip_r.at[G0 + g])
 
-    def far_up(i):
-        up_chunk(i)
-        pair_copy(1, one(i), span[FAR], pair_r.at[C0 + i]).start()
-
-    def far_add(i):
-        landed(pair_in.at[1, one(i), :, span[FAR]], pair_r.at[C0 + i])
-        add_pair(1, i, span[FAR])
-        chip_start(1, one(i), span[FAR], chip_r.at[C0 + i])
+    def far_up(g):
+        for i in range(*far_sets[g]):
+            up_chunk(i)
+        pair_copy(1, ats(far_sets[g]), span[FAR], pair_r.at[C0 + g]).start()
+
+    def far_add(g):
+        landed(pair_in.at[1, ats(far_sets[g]), :, span[FAR]], pair_r.at[C0 + g])
+        for i in range(*far_sets[g]):
+            add_pair(1, i, span[FAR])
+        chip_start(1, ats(far_sets[g]), span[FAR], chip_r.at[C0 + g])
 
     def near_pair(g):
         pair_copy(1, ats(near_sets[g]), span[NEAR], pair_r.at[N0 + g]).start()
 
-    def far_hidden(i):
-        landed(chip_in.at[1, one(i), :, span[FAR]], chip_r.at[C0 + i])
-        make_hidden(i, FAR)
-        hid_start(one(i), span[FAR], hid_r.at[C0 + i])
-
-    def far_forward(i):
-        hid_landed(one(i), span[FAR], hid_r.at[C0 + i])
-        fwd_copy(one(i), span[FAR], fwd_r.at[C0 + i]).start()
-
-    def far_down(i):
-        landed(hid_all.at[one(i), 0, :, span[FAR]], fwd_r.at[C0 + i])
-        down(i, FAR)
+    def far_hidden(g):
+        at = ats(far_sets[g])
+        landed(chip_in.at[1, at, :, span[FAR]], chip_r.at[C0 + g])
+        for i in range(*far_sets[g]):
+            make_hidden(i, FAR)
+        hid_start(at, span[FAR], hid_r.at[C0 + g])
+        if g in DIRECT:
+            cross_start(at, span[FAR], fwd_r.at[C0 + g])
+
+    def far_forward(g):
+        hid_landed(ats(far_sets[g]), span[FAR], hid_r.at[C0 + g])
+        if g not in DIRECT:
+            fwd_copy(ats(far_sets[g]), span[FAR], fwd_r.at[C0 + g]).start()
+
+    def far_down(g):
+        landed(hid_all.at[ats(far_sets[g]), 0, :, span[FAR]], fwd_r.at[C0 + g])
+        for i in range(*far_sets[g]):
+            down(i, FAR)
 
     def near_add(g):
         landed(pair_in.at[1, ats(near_sets[g]), :, span[NEAR]], pair_r.at[N0 + g])
@@ -434,21 +482,24 @@
         for i in range(count):
             ops.append((first + i * step, len(ops), f, i))
 
-    ng, nn = len(gate_sets), len(near_sets)
+    ng, nn, nf = len(gate_sets), len(near_sets), len(far_sets)
     put(gate_set, ng, -20)
     put(gate_add, ng, *T_GATE_ADD)
     put(lambda _: weights_here(1, up_vm), 1, -0.5)
-    put(far_up, nch, 0)
+    if DOWN_AT == 3:
+        put(lambda _: start_weights(2, 0, blocks), 1, -3)
+    for g, (lo, hi) in enumerate(far_sets):
+        ops.append((hi - 1.0, len(ops), far_up, g))
     for g, (lo, hi) in enumerate(near_sets):
-        ops.append((hi - 0.9, len(ops), near_pair, g))
-    put(far_add, nch, *T_FAR_ADD)
+        ops.append((nch - 0.9, len(ops), near_pair, g))
+    put(far_add, nf, *T_FAR_ADD)
     put(near_add, nn, *T_NEAR_ADD)
     put(gate_land, ng, T_FAR_HID[0] - 0.5, 0.01)
-    put(far_hidden, nch, *T_FAR_HID)
+    put(far_hidden, nf, *T_FAR_HID)
     put(near_hidden, nn, *T_NEAR_HID)
-    put(far_forward, nch, *T_FAR_FWD)
+    put(far_forward, nf, *T_FAR_FWD)
     put(down_here, 1, T_FAR_DOWN[0] - 0.05)
-    put(far_down, nch, *T_FAR_DOWN)
+    put(far_down, nf, *T_FAR_DOWN)
     end = max(t for t, *_ in ops)
     put(far_return, 1, end + 1)
     put(near_forward, nn, *T_NEAR_FWD)
@@ -496,16 +547,15 @@
     tile = rows * sub
     groups = n // mdl
     piece = 2 * batch // chips
-    marks = len(cut(nch, GATE_SETS)) + len(cut(nch, NEAR_SETS)) + nch
+    marks = len(cut(nch, GATE_SETS)) + len(cut(nch, NEAR_SETS)) + len(cut(nch, FAR_SETS))
     dims = (n, mdl, rows, heads, hd, kv, cache, width, bw, cap, cb, blocks, groups)
     dma = pltpu.SemaphoreType.DMA
     vmem = pl.BlockSpec(memory_space=pltpu.VMEM)
-    smem = pl.BlockSpec(memory_space=pltpu.SMEM)
     hbm = pl.BlockSpec(memory_space=pl.ANY)
     return pl.pallas_call(
         functools.partial(layer_kernel, dims),
         out_shape=pltpu.VMEM((rows, width), BF16),
-        in_specs=[smem] * 3 + [hbm] * 8,
+        in_specs=[hbm] * 11,
         out_specs=vmem,
         scratch_shapes=[
             pltpu.VMEM(queries.shape, BF16),
@@ -543,6 +593,10 @@
             dma((marks,)),
             dma(()),
             dma((2,)),
+            pltpu.SMEM(lengths.shape, jnp.int32),
+            pltpu.SMEM(block_list.shape, jnp.int32),
+            pltpu.SMEM(block_count.shape, jnp.int32),
+            dma((3,)),
         ],
         compiler_params=pltpu.CompilerParams(
             collective_id=0, has_side_effects=True, vmem_limit_bytes=63_000_000

time: 32.9 us -> 31.6 us (0.960)
  Pallas kernels: 32.1 us -> 30.8 us
    pallas_call x1, Pallas kernels: 32.1 us -> 30.8 us  [on_device(): pl.pallas_call(functools.partial(layer_kernel, dims), out_shape=pltpu.VME...]
where the time goes in v3:
time: 31.6 us; the launch traced here: 31.4 us
  Pallas kernels  30.8 us (97%)
  local copies, waits for them, and re-layouts  0.63 us (2%)
    pallas_call x1, Pallas kernels, on_device(): pl.pallas_call(functools.partial(layer_kernel, dims), out_shape=pltpu.VME...  30.8 us
    unnamed x1, local copies, waits for them, and re-layouts  0.63 us

profile of v3, /device:TPU:0, one launch (start us, length us, event | category | flops | bytes accessed | tf_op | source)
XLA Modules:
  0.0 31.4 jit_solution(16914473514659489875)
XLA Ops:
  0.0 30.8 %decode_layer.1 = bf16[4,8192]{1,0:T(4,128)(2,1)S(1)} custom-call(s32[4]{0:T(128)} %lengths_hbm.1, s32[2,28]{1,0:T(2,128)} %list_hbm.1, s32[2]{0:T(128)} %count_hbm.1, bf16[4,64,128]{2,1,0:T(8,128)(2,1)} %q_hbm.1, bf16[4,8192]{1,0:T(4,128)(2,1)} %res_hbm.1, f32[64,128]{1,0:T(8,128)} %bitcast.1, bf16[4,192,1024]{2,1,0:T(8,128)(2,1)} %k_hbm.1, ...), custom_call_target="tpu_custom_call" | custom-call | tf_op jit(solution)/shard_map/decode_layer/pallas_call | solution.py:555
  30.8 0.6 %copy.13 = bf16[4,8192]{1,0:T(4,128)(2,1)} copy(bf16[4,8192]{1,0:T(4,128)(2,1)S(1)} %decode_layer.1) | data formatting | bytes 131072

commit v4 on v3

--- a/solution.py
+++ b/solution.py
@@ -18,8 +18,9 @@
 FARTHEST = True
 GATE_WHOLE = True
 GATE_SETS = (2, 4)
-NEAR_SETS = (4,)
+NEAR_SETS = ()
 FAR_SETS = (1, 2, 3, 4, 5, 6)
+JOINT = 4
 DIRECT = ()
 T_GATE_ADD = (-2, 1.2)
 T_FAR_ADD = (4.5, 1)
@@ -29,6 +30,12 @@
 T_FAR_FWD = (30, 1)
 T_FAR_DOWN = (34.5, 1)
 T_NEAR_FWD = (37.9, 2)
+
+
+def near_cut(count):
+    lo = max([hi for _, hi in cut(count, FAR_SETS) if hi <= JOINT], default=0)
+    edges = [lo, *(e for e in NEAR_SETS if lo < e < count), count]
+    return [(a, b) for a, b in zip(edges[:-1], edges[1:]) if b > a]
 
 
 def cut(count, edges):
@@ -318,13 +325,14 @@
             total = total + chip_in[s, i, k - 1, row].astype(F32)
         return total
 
-    def make_hidden(i, p):
-        gate, up = total_of(0, i, span[p]), total_of(1, i, span[p])
-        row = lax.broadcasted_iota(jnp.int32, gate.shape, 0)
-        active = row < (count_ref[group] - (i * cb + core * 2)) * rp[p]
-        hid_all[i, core, chip, span[p], :] = jnp.where(
-            active, jnp.maximum(gate, 0.0) * up, 0.0
-        ).astype(BF16)
+    def make_hidden(i, which):
+        for p in which:
+            gate, up = total_of(0, i, span[p]), total_of(1, i, span[p])
+            row = lax.broadcasted_iota(jnp.int32, gate.shape, 0)
+            active = row < (count_ref[group] - (i * cb + core * 2)) * rp[p]
+            hid_all[i, core, chip, span[p], :] = jnp.where(
+                active, jnp.maximum(gate, 0.0) * up, 0.0
+            ).astype(BF16)
 
     def hid_start(at, row, sem):
         for k in range(1, chips):
@@ -345,21 +353,23 @@
         ref = hid_all.at[at, core, :, row]
         return remote(ref, ref, fwd_s, sem, partner)
 
-    def down(i, p):
-        total = acc[pl.ds(part_at[p], part_rows[p]), :]
+    def down(i, which):
+        at = pl.ds(part_at[which[0]], sum(part_rows[p] for p in which))
+        total = acc[at, :]
         for c in range(2):
             parts = []
-            for q in range(chips):
-                two = hid_all[i, c, q, span[p], :].astype(F32)
-                parts.append(jnp.concatenate([two[: rp[p]], two[rp[p] :]], axis=1))
+            for p in which:
+                for q in range(chips):
+                    two = hid_all[i, c, q, span[p], :].astype(F32)
+                    parts.append(jnp.concatenate([two[: rp[p]], two[rp[p] :]], axis=1))
             lhs = jnp.concatenate(parts, axis=0).astype(BF16)
             w = jnp.concatenate(
                 [down_vm[list_ref[group, i * cb + c * 2 + b]] for b in range(2)], axis=0
             )
             total = total + jnp.dot(lhs, w, preferred_element_type=F32)
-        acc[pl.ds(part_at[p], part_rows[p]), :] = total
-
-    gate_sets, near_sets = cut(nch, GATE_SETS), cut(nch, NEAR_SETS)
+        acc[at, :] = total
+
+    gate_sets, near_sets = cut(nch, GATE_SETS), near_cut(nch)
     G0, N0 = 0, len(gate_sets)
     far_sets = cut(nch, FAR_SETS)
     C0 = N0 + len(near_sets)
@@ -367,6 +377,12 @@
     def ats(lo_hi):
         lo, hi = lo_hi
         return pl.ds(lo, hi - lo)
+
+    def far_row(g):
+        return both if far_sets[g][1] <= JOINT else span[FAR]
+
+    def far_parts(g):
+        return (FAR, NEAR) if far_sets[g][1] <= JOINT else (FAR,)
 
     def gate_set(g):
         for i in range(*gate_sets[g]):
@@ -388,35 +404,35 @@
     def far_up(g):
         for i in range(*far_sets[g]):
             up_chunk(i)
-        pair_copy(1, ats(far_sets[g]), span[FAR], pair_r.at[C0 + g]).start()
+        pair_copy(1, ats(far_sets[g]), far_row(g), pair_r.at[C0 + g]).start()
 
     def far_add(g):
-        landed(pair_in.at[1, ats(far_sets[g]), :, span[FAR]], pair_r.at[C0 + g])
+        landed(pair_in.at[1, ats(far_sets[g]), :, far_row(g)], pair_r.at[C0 + g])
         for i in range(*far_sets[g]):
-            add_pair(1, i, span[FAR])
-        chip_start(1, ats(far_sets[g]), span[FAR], chip_r.at[C0 + g])
+            add_pair(1, i, far_row(g))
+        chip_start(1, ats(far_sets[g]), far_row(g), chip_r.at[C0 + g])
 
     def near_pair(g):
         pair_copy(1, ats(near_sets[g]), span[NEAR], pair_r.at[N0 + g]).start()
 
     def far_hidden(g):
         at = ats(far_sets[g])
-        landed(chip_in.at[1, at, :, span[FAR]], chip_r.at[C0 + g])
+        landed(chip_in.at[1, at, :, far_row(g)], chip_r.at[C0 + g])
         for i in range(*far_sets[g]):
-            make_hidden(i, FAR)
-        hid_start(at, span[FAR], hid_r.at[C0 + g])
+            make_hidden(i, far_parts(g))
+        hid_start(at, far_row(g), hid_r.at[C0 + g])
         if g in DIRECT:
-            cross_start(at, span[FAR], fwd_r.at[C0 + g])
+            cross_start(at, far_row(g), fwd_r.at[C0 + g])
 
     def far_forward(g):
-        hid_landed(ats(far_sets[g]), span[FAR], hid_r.at[C0 + g])
+        hid_landed(ats(far_sets[g]), far_row(g), hid_r.at[C0 + g])
         if g not in DIRECT:
-            fwd_copy(ats(far_sets[g]), span[FAR], fwd_r.at[C0 + g]).start()
+            fwd_copy(ats(far_sets[g]), far_row(g), fwd_r.at[C0 + g]).start()
 
     def far_down(g):
-        landed(hid_all.at[ats(far_sets[g]), 0, :, span[FAR]], fwd_r.at[C0 + g])
+        landed(hid_all.at[ats(far_sets[g]), 0, :, far_row(g)], fwd_r.at[C0 + g])
         for i in range(*far_sets[g]):
-            down(i, FAR)
+            down(i, far_parts(g))
 
     def near_add(g):
         landed(pair_in.at[1, ats(near_sets[g]), :, span[NEAR]], pair_r.at[N0 + g])
@@ -425,7 +441,7 @@
 
     def near_hidden(g):
         landed(chip_in.at[1, ats(near_sets[g]), :, span[NEAR]], chip_r.at[N0 + g])
-        loop(*near_sets[g], lambda i: make_hidden(i, NEAR))
+        loop(*near_sets[g], lambda i: make_hidden(i, (NEAR,)))
         hid_start(ats(near_sets[g]), span[NEAR], hid_r.at[N0 + g])
 
     def near_forward(g):
@@ -434,7 +450,7 @@
 
     def near_down(g):
         landed(hid_all.at[ats(near_sets[g]), 0, :, span[NEAR]], fwd_r.at[N0 + g])
-        loop(*near_sets[g], lambda i: down(i, NEAR))
+        loop(*near_sets[g], lambda i: down(i, (NEAR,)))
 
     def down_here(_):
         weights_here(2, down_vm)
@@ -454,14 +470,14 @@
 
     def far_return(_):
         spread(FAR)
-        loop(0, far_n, narrow)
-        loop(
-            0,
-            far_n,
-            lambda k: remote(
+
+        def send(k):
+            narrow(far_slot(k))
+            remote(
                 ret_out.at[far_slot(k)], ret_in.at[me], ret_s, ret_r.at[FAR], far_dev(k)
-            ).start(),
-        )
+            ).start()
+
+        loop(0, far_n, send)
 
     def near_return(_):
         spread(NEAR)
@@ -547,7 +563,7 @@
     tile = rows * sub
     groups = n // mdl
     piece = 2 * batch // chips
-    marks = len(cut(nch, GATE_SETS)) + len(cut(nch, NEAR_SETS)) + len(cut(nch, FAR_SETS))
+    marks = len(cut(nch, GATE_SETS)) + len(near_cut(nch)) + len(cut(nch, FAR_SETS))
     dims = (n, mdl, rows, heads, hd, kv, cache, width, bw, cap, cb, blocks, groups)
     dma = pltpu.SemaphoreType.DMA
     vmem = pl.BlockSpec(memory_space=pltpu.VMEM)

time: 31.6 us -> 31.1 us (0.984)
  Pallas kernels: 30.8 us -> 30.3 us
    pallas_call x1, Pallas kernels: 30.8 us -> 30.3 us  [on_device(): pl.pallas_call(functools.partial(layer_kernel, dims), out_shape=pltpu.VME...]
where the time goes in v4:
time: 31.1 us; the launch traced here: 30.9 us
  Pallas kernels  30.3 us (97%)
  local copies, waits for them, and re-layouts  0.63 us (2%)
    pallas_call x1, Pallas kernels, on_device(): pl.pallas_call(functools.partial(layer_kernel, dims), out_shape=pltpu.VME...  30.3 us
    unnamed x1, local copies, waits for them, and re-layouts  0.63 us

profile of v4, /device:TPU:0, one launch (start us, length us, event | category | flops | bytes accessed | tf_op | source)
XLA Modules:
  0.0 30.9 jit_solution(9843175995783921593)
XLA Ops:
  0.0 30.3 %decode_layer.1 = bf16[4,8192]{1,0:T(4,128)(2,1)S(1)} custom-call(s32[4]{0:T(128)} %lengths_hbm.1, s32[2,28]{1,0:T(2,128)} %list_hbm.1, s32[2]{0:T(128)} %count_hbm.1, bf16[4,64,128]{2,1,0:T(8,128)(2,1)} %q_hbm.1, bf16[4,8192]{1,0:T(4,128)(2,1)} %res_hbm.1, f32[64,128]{1,0:T(8,128)} %bitcast.1, bf16[4,192,1024]{2,1,0:T(8,128)(2,1)} %k_hbm.1, ...), custom_call_target="tpu_custom_call" | custom-call | tf_op jit(solution)/shard_map/decode_layer/pallas_call | solution.py:571
  30.3 0.6 %copy.13 = bf16[4,8192]{1,0:T(4,128)(2,1)} copy(bf16[4,8192]{1,0:T(4,128)(2,1)S(1)} %decode_layer.1) | data formatting | bytes 131072
